TPU v7x, 32 devices: a whole 2x2x4 slice. The times are simulated.
32 devices in a mesh: rep: 2 (over x), dp: 16 (over y, z, core).
Axes of the slice: x: 2, y: 2, z: 4, core: 2. Of those that a mesh axis runs over, the one named last changes fastest.
Arguments:
- x: bfloat16 [32, 2048, 640], P(('rep', 'dp')), parts along dimension 0
- dy: bfloat16 [32, 2048, 640], P(('rep', 'dp')), parts along dimension 0
- w_gate: bfloat16 [2, 640, 2560], replicated
- w_up: bfloat16 [2, 640, 2560], replicated
- w_down: bfloat16 [2, 2560, 640], replicated
- m_w_gate: float32 [2, 640, 2560], P(None, 'dp')
- m_w_up: float32 [2, 640, 2560], P(None, 'dp')
- m_w_down: float32 [2, 2560, 640], P(None, 'dp')
- v_w_gate: float32 [2, 640, 2560], P(None, 'dp')
- v_w_up: float32 [2, 640, 2560], P(None, 'dp')
- v_w_down: float32 [2, 2560, 640], P(None, 'dp')
Outputs:
- output 1: bfloat16 [4, 640, 2560], P('rep'), parts along dimension 0
- output 2: bfloat16 [4, 640, 2560], P('rep'), parts along dimension 0
- output 3: bfloat16 [4, 2560, 640], P('rep'), parts along dimension 0
- output 4: float32 [4, 640, 2560], P('rep', 'dp'), parts along dimension 0
- output 5: float32 [4, 640, 2560], P('rep', 'dp'), parts along dimension 0
- output 6: float32 [4, 2560, 640], P('rep', 'dp'), parts along dimension 0
- output 7: float32 [4, 640, 2560], P('rep', 'dp'), parts along dimension 0
- output 8: float32 [4, 640, 2560], P('rep', 'dp'), parts along dimension 0
- output 9: float32 [4, 2560, 640], P('rep', 'dp'), parts along dimension 0
There are 2 independent parts. A program takes and returns all parts, laid end to end along the dimension named above; an argument that names none is the same for every part.
All inputs are finite; a program needn't handle non-finite values.
Results may differ from a plain program's by a relative error of at most 0.022.
Values are sent between devices in bfloat16 or wider.
A program may use at most 2 GiB of HBM per device.

v0:
```python
import jax
import jax.numpy as jnp
from jax import lax

NAMES = ("w_gate", "w_up", "w_down")


def matmul(a, w):
    return jnp.dot(a, w, preferred_element_type=jnp.float32).astype(jnp.bfloat16)


def normed(h):
    wide = h.astype(jnp.float32)
    scale = lax.rsqrt(jnp.mean(wide**2, -1, keepdims=True) + 1e-6)
    return (wide * scale).astype(jnp.bfloat16)


def layer(h, w):
    a = normed(h)
    gate = jnp.dot(a, w["w_gate"], preferred_element_type=jnp.float32)
    up = jnp.dot(a, w["w_up"], preferred_element_type=jnp.float32)
    return h + matmul((jax.nn.silu(gate) * up).astype(jnp.bfloat16), w["w_down"])


def adamw(w, m, v, g):
    m = 0.9 * m + 0.1 * g
    v = 0.95 * v + 0.05 * g * g
    step = m * lax.rsqrt(v + 1e-8) + 0.1 * w
    return (w - 0.02 * step).astype(jnp.bfloat16), m, v


def stack(weights, h):
    for number in range(weights["w_gate"].shape[0]):
        h = layer(h, {name: w[number] for name, w in weights.items()})
    return h


def solution(mesh):
    groups = mesh.shape["rep"]

    def step(x, dy, *arrays):
        weights, m, v = (arrays[i : i + 3] for i in (0, 3, 6))
        x, dy = (t.reshape(groups, -1, *t.shape[1:]) for t in (x, dy))

        def of_a_group(x, dy):
            _, back = jax.vjp(lambda w: stack(w, x), dict(zip(NAMES, weights, strict=True)))
            by_weights = back(dy)[0]
            gradients = [by_weights[name].astype(jnp.float32) for name in NAMES]
            new = [adamw(w.astype(jnp.float32), m, v, g) for w, m, v, g in zip(weights, m, v, gradients, strict=True)]
            return tuple(one[which] for which in range(3) for one in new)

        return tuple(t.reshape(-1, *t.shape[2:]) for t in jax.vmap(of_a_group)(x, dy))

    return step
```

profile of v0, /device:TPU:0, one launch (start us, length us, event | category | flops | bytes accessed | tf_op | source)
XLA Modules:
  0.0 1140.0 jit_solution(13096104065873676390)
XLA Ops:
  16.7 12.6 %convolution_convert_fusion.1 = bf16[2048,2560]{1,0:T(8,128)(2,1)} fusion(bf16[2,2560,640]{2,1,0:T(8,128)(2,1)} %param.16, bf16[1,2048,640]{2,1,0:T(8,128)(2,1)S(1)} %copy-done.21), kind=kOutput, calls=%fused_computation.199 | convolution fusion | flops 6716129280 | bytes 16384000 | tf_op jit(solution)/vmap(transpose(jvp()))/dot_general | solution.py:9
  29.4 13.9 %fusion.188 = f32[2048,2560]{1,0:T(8,128)} fusion(bf16[2,640,2560]{2,1,0:T(8,128)(2,1)} %param.12, bf16[1,2048,640]{2,1,0:T(8,128)(2,1)S(1)} %copy-done.17, f32[2048]{0:T(1024)S(1)} %add_rsqrt_fusion), kind=kOutput, calls=%fused_computation.228 | convolution fusion | flops 6714818560 | bytes 26877952 | tf_op jit(solution)/vmap(jvp())/dot_general | solution.py:20
  43.3 21.9 %fusion.164 = (bf16[1,1,2048,2560]{3,2,1,0:T(8,128)(2,1)S(1)}, f32[2048,2560]{1,0:T(8,128)}) fusion(f32[2048,2560]{1,0:T(8,128)} %fusion.188, bf16[2,640,2560]{2,1,0:T(8,128)(2,1)} %param.15, bf16[1,2048,640]{2,1,0:T(8,128)(2,1)} %param.14, f32[2048]{0:T(1024)S(1)} %add_rsqrt_fusion), kind=kOutput, calls=%fused_computation.191 | convolution fusion | flops 6746275840 | bytes 58335232 | tf_op jit(solution)/vmap(jvp())/dot_general | solution.py:21
  65.2 13.5 %fusion.174 = (f32[2048]{0:T(1024)S(1)}, bf16[1,1,2048,640]{2,3,1,0:T(8,128)(2,1)S(1)}) fusion(bf16[2,2560,640]{2,1,0:T(8,128)(2,1)} %param.16, bf16[1,1,2048,2560]{3,2,1,0:T(8,128)(2,1)S(1)} %get-tuple-element.263, bf16[1,2048,640]{1,2,0:T(8,128)(2,1)} %copy), kind=kOutput, calls=%fused_computation.213 | convolution fusion | flops 6717437952 | bytes 19013632 | tf_op jit(solution)/vmap(jvp())/dot_general | solution.py:9
  80.9 15.3 %fusion.180 = f32[2048,2560]{1,0:T(8,128)} fusion(bf16[2,640,2560]{2,1,0:T(8,128)(2,1)} %param.15, bf16[1,1,2048,640]{2,3,1,0:T(8,128)(2,1)S(1)} %fusion.175), kind=kOutput, calls=%fused_computation.220 | convolution fusion | flops 6710886400 | bytes 26869760 | tf_op jit(solution)/vmap(jvp())/dot_general | solution.py:21
  96.2 30.3 %fusion.153 = (bf16[1,1,2048,2560]{3,2,1,0:T(8,128)(2,1)}, bf16[1,1,2048,2560]{3,2,1,0:T(8,128)(2,1)}, f32[2048,2560]{1,0:T(8,128)}) fusion(f32[2048,2560]{1,0:T(8,128)} %fusion.180, bf16[2048,2560]{1,0:T(8,128)(2,1)} %convolution_convert_fusion.1, bf16[2,640,2560]{2,1,0:T(8,128)(2,1)S(1)} %bitcast.674, bf16[1,1,2048,640]{2,3,1,0:T(8,128)(2,1)S(1)} %fusion.175), kind=kOutput, calls=%fused_computation.175 | convolution fusion | flops 6789529600 | bytes 79298560 | tf_op jit(solution)/vmap(jvp())/dot_general | solution.py:20
  126.5 19.4 %fusion.163 = bf16[1,1,2048,2560]{3,2,1,0:T(8,128)(2,1)} fusion(f32[2048,2560]{1,0:T(8,128)} %fusion.180, f32[2048,2560]{1,0:T(8,128)} %get-tuple-element.267), kind=kLoop, calls=%fused_computation.189 | loop fusion | flops 31457280 | bytes 52428800 | tf_op jit(solution)/vmap(jvp())/convert_element_type | solution.py:22
  145.9 14.6 %copy.2 = bf16[1,1,2048,2560]{2,3,1,0:T(8,128)(2,1)} copy(bf16[1,1,2048,2560]{3,2,1,0:T(8,128)(2,1)} %fusion.163) | data formatting | bytes 20971520
  163.7 126.3 %while.16 = (bf16[1,1,2048,2560]{2,3,1,0:T(8,128)(2,1)}, bf16[1,1,2048,640]{3,2,1,0:T(8,128)(2,1)S(1)}, f32[1,160,640]{2,1,0:T(8,128)S(1)}, f32[1,160,640]{2,1,0...) while((bf16[1,1,2048,2560]{2,3,1,0:T(8,128)(2,1)}, ...), condition=%wide.windowed_dot_general_cond_rs.4.clone, body=%wide.windowed_dot_general_body_rs.4.clone.sunk | while | flops 1683578880 | bytes 40960612 | solution.py:9
  290.0 15.0 %copy.4 = bf16[1,1,2048,2560]{2,3,1,0:T(8,128)(2,1)} copy(bf16[1,1,2048,2560]{3,2,1,0:T(8,128)(2,1)} %copy-done.16) | data formatting | bytes 20971520
  305.0 10.8 fusion.198
  315.9 9.1 fusion.176
  331.5 132.2 %while.17 = (bf16[1,1,2048,2560]{2,3,1,0:T(8,128)(2,1)}, bf16[1,1,2048,640]{3,2,1,0:T(8,128)(2,1)S(1)}, f32[1,160,640]{2,1,0:T(8,128)S(1)}, f32[1,160,640]{2,1,0...) while((bf16[1,1,2048,2560]{2,3,1,0:T(8,128)(2,1)}, ...), condition=%wide.windowed_dot_general_cond_rs.5.clone, body=%wide.windowed_dot_general_body_rs.5.clone.sunk | while | flops 1683578880 | bytes 44237468 | solution.py:9
  464.5 116.8 %while.14 = (bf16[1,1,2048,640]{2,3,1,0:T(8,128)(2,1)}, bf16[1,1,2048,2560]{3,2,1,0:T(8,128)(2,1)}, f32[1,40,2560]{2,1,0:T(8,128)S(1)}, f32[1,40,2560]{2,1,0:T(8...) while((bf16[1,1,2048,640]{2,3,1,0:T(8,128)(2,1)}, ...), condition=%wide.windowed_dot_general_cond_rs.2.clone, body=%wide.windowed_dot_general_body_rs.2.clone.sunk | while | flops 1679646720 | bytes 82903744 | solution.py:21
  586.0 28.9 %convert_multiply_fusion = (bf16[1,1,2048,2560]{3,2,1,0:T(8,128)(2,1)}, bf16[1,1,2048,2560]{3,2,1,0:T(8,128)(2,1)}) fusion(f32[2048,2560]{1,0:T(8,128)} %fusion.188, f32[2048,2560]{1,0:T(8,128)} %get-tuple-element.264, bf16[2,2560,640]{2,1,0:T(8,128)(2,1)} %param.16, bf16[1,1,2048,640]{2,3,1,0:T(8,128)(2,1)} %fusion.219), kind=kOutput, calls=%fused_computation.170 | convolution fusion | flops 6794772480 | bytes 68812800 | tf_op jit(solution)/vmap(transpose(jvp()))/dot_general | solution.py:9
  614.9 119.2 %while.15 = (bf16[1,1,2048,640]{2,3,1,0:T(8,128)(2,1)}, bf16[1,1,2048,2560]{3,2,1,0:T(8,128)(2,1)}, f32[1,40,2560]{2,1,0:T(8,128)S(1)}, f32[1,40,2560]{2,1,0:T(8...) while((bf16[1,1,2048,640]{2,3,1,0:T(8,128)(2,1)}, ...), condition=%wide.windowed_dot_general_cond_rs.3.clone, body=%wide.windowed_dot_general_body_rs.3.clone.sunk | while | flops 1679646720 | bytes 82903744 | solution.py:21
  741.6 146.5 %while.12 = (bf16[1,1,2048,640]{2,3,1,0:T(8,128)(2,1)}, bf16[1,1,2048,2560]{3,2,1,0:T(8,128)(2,1)}, f32[1,40,2560]{2,1,0:T(8,128)S(1)}, f32[1,40,2560]{2,1,0:T(8...) while((bf16[1,1,2048,640]{2,3,1,0:T(8,128)(2,1)}, ...), condition=%wide.windowed_dot_general_cond_rs.clone, body=%wide.windowed_dot_general_body_rs.clone.sunk | while | flops 1679646720 | bytes 82903744 | solution.py:20
  763.4 12.7 %collective-permute-done.2 = f32[1,40,2560]{2,1,0:T(8,128)S(1)} collective-permute-done((f32[1,40,2560]{2,1,0:T(8,128)S(1)}, f32[1,40,2560]{2,1,0:T(8,128)S(1)}, u32[]{:S(2)}, u32[]{:S(2)}) %collective-permute-start.2) | collective-permute-done | bytes 409632 | tf_op jit(solution)/vmap(transpose(jvp()))/dot_general | solution.py:20
  803.1 16.6 %collective-permute-done.2 = f32[1,40,2560]{2,1,0:T(8,128)S(1)} collective-permute-done((f32[1,40,2560]{2,1,0:T(8,128)S(1)}, f32[1,40,2560]{2,1,0:T(8,128)S(1)}, u32[]{:S(2)}, u32[]{:S(2)}) %collective-permute-start.2) | collective-permute-done | bytes 409632 | tf_op jit(solution)/vmap(transpose(jvp()))/dot_general | solution.py:20
  822.5 11.7 %collective-permute-start = (f32[1,40,2560]{2,1,0:T(8,128)}, f32[1,40,2560]{2,1,0:T(8,128)S(1)}, u32[]{:S(2)}, u32[]{:S(2)}) collective-permute-start(f32[1,40,2560]{2,1,0:T(8,128)} %broadcast_select_fusion.24), channel_id=3, source_target_pairs={{0,1},{1,2},{2,3},{3,4},{4,5},{5,6},{6,7},{7,8},{8,9},{9,10},{10,1... | collective-permute-start | bytes 1228808 | tf_op jit(solution)/vmap(transpose(jvp()))/dot_general | solution.py:20
  893.7 145.5 %while.13 = (bf16[1,1,2048,640]{2,3,1,0:T(8,128)(2,1)}, bf16[1,1,2048,2560]{3,2,1,0:T(8,128)(2,1)}, f32[1,40,2560]{2,1,0:T(8,128)S(1)}, f32[1,40,2560]{2,1,0:T(8...) while((bf16[1,1,2048,640]{2,3,1,0:T(8,128)(2,1)}, ...), condition=%wide.windowed_dot_general_cond_rs.1.clone, body=%wide.windowed_dot_general_body_rs.1.clone.sunk | while | flops 1679646720 | bytes 82903744 | solution.py:20
  914.7 15.5 %collective-permute-done.6 = f32[1,40,2560]{2,1,0:T(8,128)S(1)} collective-permute-done((f32[1,40,2560]{2,1,0:T(8,128)S(1)}, f32[1,40,2560]{2,1,0:T(8,128)S(1)}, u32[]{:S(2)}, u32[]{:S(2)}) %collective-permute-start.6) | collective-permute-done | bytes 409632 | tf_op jit(solution)/vmap(transpose(jvp()))/dot_general | solution.py:20
  960.1 13.9 %collective-permute-done.6 = f32[1,40,2560]{2,1,0:T(8,128)S(1)} collective-permute-done((f32[1,40,2560]{2,1,0:T(8,128)S(1)}, f32[1,40,2560]{2,1,0:T(8,128)S(1)}, u32[]{:S(2)}, u32[]{:S(2)}) %collective-permute-start.6) | collective-permute-done | bytes 409632 | tf_op jit(solution)/vmap(transpose(jvp()))/dot_general | solution.py:20
  1052.6 66.2 %all-gather.10.cloned.1.call-done = bf16[1,2,640,2560]{3,2,1,0:T(8,128)(2,1)} async-done(((bf16[1,2,40,2560]{3,2,1,0:T(8,128)(2,1)}), bf16[1,2,640,2560]{3,2,1,0:T(8,128)(2,1)}) %all-gather.10.cloned.1.call-update) | async-done | bytes 6553616 | tf_op jit(solution)/reshape | solution.py:52
  (635 shorter events, 736.7 us)
Async XLA Ops:
  7.2 1045.3 %all-gather.14.cloned.1.call-start = ((), (), s32[]{:S(2)}) async-start(), calls=%async_computation.2 | async-start | bytes 6963200 | tf_op jit(solution)/reshape | solution.py:52
  290.0 446.2 %collective-permute-start.28 = (f32[1,160,640]{2,1,0:T(8,128)}, f32[1,160,640]{2,1,0:T(8,128)}, u32[]{:S(2)}, u32[]{:S(2)}) collective-permute-start(f32[1,160,640]{2,1,0:T(8,128)} %get-tuple-element.45), channel_id=32, source_target_pairs={{0,1},{1,2},{2,3},{3,4},{4,5},{5,6},{6,7},{7,8},{8,9},{9,10},{10,1... | collective-permute-start | bytes 1228808 | tf_op jit(solution)/vmap(transpose(jvp()))/dot_general | solution.py:9
  346.8 14.7 %collective-permute-start.23 = (f32[1,160,640]{2,1,0:T(8,128)S(1)}, f32[1,160,640]{2,1,0:T(8,128)}, u32[]{:S(2)}, u32[]{:S(2)}) collective-permute-start(f32[1,160,640]{2,1,0:T(8,128)S(1)} %get-tuple-element.501), channel_id=36, source_target_pairs={{0,15},{1,0},{2,1},{3,2},{4,3},{5,4},{6,5},{7,6},{8,7},{9,8},{10,9... | collective-permute-start | bytes 1228808 | tf_op jit(solution)/vmap(transpose(jvp()))/dot_general | solution.py:9
  446.8 14.9 %collective-permute-start.23 = (f32[1,160,640]{2,1,0:T(8,128)S(1)}, f32[1,160,640]{2,1,0:T(8,128)}, u32[]{:S(2)}, u32[]{:S(2)}) collective-permute-start(f32[1,160,640]{2,1,0:T(8,128)S(1)} %get-tuple-element.501), channel_id=36, source_target_pairs={{0,15},{1,0},{2,1},{3,2},{4,3},{5,4},{6,5},{7,6},{8,7},{9,8},{10,9... | collective-permute-start | bytes 1228808 | tf_op jit(solution)/vmap(transpose(jvp()))/dot_general | solution.py:9
  463.7 273.5 %collective-permute-start.29 = (f32[1,160,640]{2,1,0:T(8,128)}, f32[1,160,640]{2,1,0:T(8,128)}, u32[]{:S(2)}, u32[]{:S(2)}) collective-permute-start(f32[1,160,640]{2,1,0:T(8,128)} %get-tuple-element.47), channel_id=38, source_target_pairs={{0,1},{1,2},{2,3},{3,4},{4,5},{5,6},{6,7},{7,8},{8,9},{9,10},{10,1... | collective-permute-start | bytes 1228808 | tf_op jit(solution)/vmap(transpose(jvp()))/dot_general | solution.py:9
  465.5 17.1 %collective-permute-start.8 = (f32[1,40,2560]{2,1,0:T(8,128)}, f32[1,40,2560]{2,1,0:T(8,128)S(1)}, u32[]{:S(2)}, u32[]{:S(2)}) collective-permute-start(f32[1,40,2560]{2,1,0:T(8,128)} %broadcast_select_fusion.28), channel_id=16, source_target_pairs={{0,1},{1,2},{2,3},{3,4},{4,5},{5,6},{6,7},{7,8},{8,9},{9,10},{10,1... | collective-permute-start | bytes 1228808 | tf_op jit(solution)/vmap(transpose(jvp()))/dot_general | solution.py:21
  466.2 16.3 %collective-permute-start.9 = (f32[1,40,2560]{2,1,0:T(8,128)}, f32[1,40,2560]{2,1,0:T(8,128)S(1)}, u32[]{:S(2)}, u32[]{:S(2)}) collective-permute-start(f32[1,40,2560]{2,1,0:T(8,128)} %broadcast_select_fusion.29), channel_id=15, source_target_pairs={{0,15},{1,0},{2,1},{3,2},{4,3},{5,4},{6,5},{7,6},{8,7},{9,8},{10,9... | collective-permute-start | bytes 1228808 | tf_op jit(solution)/vmap(transpose(jvp()))/dot_general | solution.py:21
  581.3 306.8 %collective-permute-start.26 = (f32[1,40,2560]{2,1,0:T(8,128)}, f32[1,40,2560]{2,1,0:T(8,128)}, u32[]{:S(2)}, u32[]{:S(2)}) collective-permute-start(f32[1,40,2560]{2,1,0:T(8,128)} %get-tuple-element.41), channel_id=19, source_target_pairs={{0,1},{1,2},{2,3},{3,4},{4,5},{5,6},{6,7},{7,8},{8,9},{9,10},{10,1... | collective-permute-start | bytes 1228808 | tf_op jit(solution)/vmap(transpose(jvp()))/dot_general | solution.py:21
  734.0 155.2 %collective-permute-start.27 = (f32[1,40,2560]{2,1,0:T(8,128)}, f32[1,40,2560]{2,1,0:T(8,128)}, u32[]{:S(2)}, u32[]{:S(2)}) collective-permute-start(f32[1,40,2560]{2,1,0:T(8,128)} %get-tuple-element.43), channel_id=25, source_target_pairs={{0,1},{1,2},{2,3},{3,4},{4,5},{5,6},{6,7},{7,8},{8,9},{9,10},{10,1... | collective-permute-start | bytes 1228808 | tf_op jit(solution)/vmap(transpose(jvp()))/dot_general | solution.py:21
  741.5 311.0 %all-gather.12.cloned.1.call-start = ((), (), s32[]{:S(2)}) async-start(), calls=%async_computation.1 | async-start | bytes 6963200 | tf_op jit(solution)/reshape | solution.py:52
  757.0 19.2 %collective-permute-start.2 = (f32[1,40,2560]{2,1,0:T(8,128)S(1)}, f32[1,40,2560]{2,1,0:T(8,128)S(1)}, u32[]{:S(2)}, u32[]{:S(2)}) collective-permute-start(f32[1,40,2560]{2,1,0:T(8,128)S(1)} %get-tuple-element.455), channel_id=5, source_target_pairs={{0,1},{1,2},{2,3},{3,4},{4,5},{5,6},{6,7},{7,8},{8,9},{9,10},{10,1... | collective-permute-start | bytes 1228808 | tf_op jit(solution)/vmap(transpose(jvp()))/dot_general | solution.py:20
  757.0 19.2 %collective-permute-start.3 = (f32[1,40,2560]{2,1,0:T(8,128)S(1)}, f32[1,40,2560]{2,1,0:T(8,128)S(1)}, u32[]{:S(2)}, u32[]{:S(2)}) collective-permute-start(f32[1,40,2560]{2,1,0:T(8,128)S(1)} %get-tuple-element.456), channel_id=4, source_target_pairs={{0,15},{1,0},{2,1},{3,2},{4,3},{5,4},{6,5},{7,6},{8,7},{9,8},{10,9... | collective-permute-start | bytes 1228808 | tf_op jit(solution)/vmap(transpose(jvp()))/dot_general | solution.py:20
  779.0 14.8 %collective-permute-start = (f32[1,40,2560]{2,1,0:T(8,128)}, f32[1,40,2560]{2,1,0:T(8,128)S(1)}, u32[]{:S(2)}, u32[]{:S(2)}) collective-permute-start(f32[1,40,2560]{2,1,0:T(8,128)} %broadcast_select_fusion.24), channel_id=3, source_target_pairs={{0,1},{1,2},{2,3},{3,4},{4,5},{5,6},{6,7},{7,8},{8,9},{9,10},{10,1... | collective-permute-start | bytes 1228808 | tf_op jit(solution)/vmap(transpose(jvp()))/dot_general | solution.py:20
  796.4 23.3 %collective-permute-start.2 = (f32[1,40,2560]{2,1,0:T(8,128)S(1)}, f32[1,40,2560]{2,1,0:T(8,128)S(1)}, u32[]{:S(2)}, u32[]{:S(2)}) collective-permute-start(f32[1,40,2560]{2,1,0:T(8,128)S(1)} %get-tuple-element.455), channel_id=5, source_target_pairs={{0,1},{1,2},{2,3},{3,4},{4,5},{5,6},{6,7},{7,8},{8,9},{9,10},{10,1... | collective-permute-start | bytes 1228808 | tf_op jit(solution)/vmap(transpose(jvp()))/dot_general | solution.py:20
  796.5 23.2 %collective-permute-start.3 = (f32[1,40,2560]{2,1,0:T(8,128)S(1)}, f32[1,40,2560]{2,1,0:T(8,128)S(1)}, u32[]{:S(2)}, u32[]{:S(2)}) collective-permute-start(f32[1,40,2560]{2,1,0:T(8,128)S(1)} %get-tuple-element.456), channel_id=4, source_target_pairs={{0,15},{1,0},{2,1},{3,2},{4,3},{5,4},{6,5},{7,6},{8,7},{9,8},{10,9... | collective-permute-start | bytes 1228808 | tf_op jit(solution)/vmap(transpose(jvp()))/dot_general | solution.py:20
  822.5 21.4 %collective-permute-start = (f32[1,40,2560]{2,1,0:T(8,128)}, f32[1,40,2560]{2,1,0:T(8,128)S(1)}, u32[]{:S(2)}, u32[]{:S(2)}) collective-permute-start(f32[1,40,2560]{2,1,0:T(8,128)} %broadcast_select_fusion.24), channel_id=3, source_target_pairs={{0,1},{1,2},{2,3},{3,4},{4,5},{5,6},{6,7},{7,8},{8,9},{9,10},{10,1... | collective-permute-start | bytes 1228808 | tf_op jit(solution)/vmap(transpose(jvp()))/dot_general | solution.py:20
  888.1 151.0 %collective-permute-start.24 = (f32[1,40,2560]{2,1,0:T(8,128)}, f32[1,40,2560]{2,1,0:T(8,128)}, u32[]{:S(2)}, u32[]{:S(2)}) collective-permute-start(f32[1,40,2560]{2,1,0:T(8,128)} %get-tuple-element.37), channel_id=6, source_target_pairs={{0,1},{1,2},{2,3},{3,4},{4,5},{5,6},{6,7},{7,8},{8,9},{9,10},{10,1... | collective-permute-start | bytes 1228808 | tf_op jit(solution)/vmap(transpose(jvp()))/dot_general | solution.py:20
  893.6 225.2 %all-gather.10.cloned.1.call-start = ((), (), s32[]{:S(2)}) async-start(), calls=%async_computation | async-start | bytes 6963200 | tf_op jit(solution)/reshape | solution.py:52
  908.3 21.9 %collective-permute-start.6 = (f32[1,40,2560]{2,1,0:T(8,128)S(1)}, f32[1,40,2560]{2,1,0:T(8,128)S(1)}, u32[]{:S(2)}, u32[]{:S(2)}) collective-permute-start(f32[1,40,2560]{2,1,0:T(8,128)S(1)} %get-tuple-element.464), channel_id=11, source_target_pairs={{0,1},{1,2},{2,3},{3,4},{4,5},{5,6},{6,7},{7,8},{8,9},{9,10},{10,1... | collective-permute-start | bytes 1228808 | tf_op jit(solution)/vmap(transpose(jvp()))/dot_general | solution.py:20
  910.8 19.7 %collective-permute-start.7 = (f32[1,40,2560]{2,1,0:T(8,128)S(1)}, f32[1,40,2560]{2,1,0:T(8,128)S(1)}, u32[]{:S(2)}, u32[]{:S(2)}) collective-permute-start(f32[1,40,2560]{2,1,0:T(8,128)S(1)} %get-tuple-element.465), channel_id=10, source_target_pairs={{0,15},{1,0},{2,1},{3,2},{4,3},{5,4},{6,5},{7,6},{8,7},{9,8},{10,9... | collective-permute-start | bytes 1228808 | tf_op jit(solution)/vmap(transpose(jvp()))/dot_general | solution.py:20
  936.0 17.3 %collective-permute-start.5 = (f32[1,40,2560]{2,1,0:T(8,128)}, f32[1,40,2560]{2,1,0:T(8,128)S(1)}, u32[]{:S(2)}, u32[]{:S(2)}) collective-permute-start(f32[1,40,2560]{2,1,0:T(8,128)} %broadcast_select_fusion.27), channel_id=8, source_target_pairs={{0,15},{1,0},{2,1},{3,2},{4,3},{5,4},{6,5},{7,6},{8,7},{9,8},{10,9... | collective-permute-start | bytes 1228808 | tf_op jit(solution)/vmap(transpose(jvp()))/dot_general | solution.py:20
  953.4 20.6 %collective-permute-start.6 = (f32[1,40,2560]{2,1,0:T(8,128)S(1)}, f32[1,40,2560]{2,1,0:T(8,128)S(1)}, u32[]{:S(2)}, u32[]{:S(2)}) collective-permute-start(f32[1,40,2560]{2,1,0:T(8,128)S(1)} %get-tuple-element.464), channel_id=11, source_target_pairs={{0,1},{1,2},{2,3},{3,4},{4,5},{5,6},{6,7},{7,8},{8,9},{9,10},{10,1... | collective-permute-start | bytes 1228808 | tf_op jit(solution)/vmap(transpose(jvp()))/dot_general | solution.py:20
  956.2 19.7 %collective-permute-start.7 = (f32[1,40,2560]{2,1,0:T(8,128)S(1)}, f32[1,40,2560]{2,1,0:T(8,128)S(1)}, u32[]{:S(2)}, u32[]{:S(2)}) collective-permute-start(f32[1,40,2560]{2,1,0:T(8,128)S(1)} %get-tuple-element.465), channel_id=10, source_target_pairs={{0,15},{1,0},{2,1},{3,2},{4,3},{5,4},{6,5},{7,6},{8,7},{9,8},{10,9... | collective-permute-start | bytes 1228808 | tf_op jit(solution)/vmap(transpose(jvp()))/dot_general | solution.py:20
  978.7 16.3 %collective-permute-start.4 = (f32[1,40,2560]{2,1,0:T(8,128)}, f32[1,40,2560]{2,1,0:T(8,128)S(1)}, u32[]{:S(2)}, u32[]{:S(2)}) collective-permute-start(f32[1,40,2560]{2,1,0:T(8,128)} %broadcast_select_fusion.26), channel_id=9, source_target_pairs={{0,1},{1,2},{2,3},{3,4},{4,5},{5,6},{6,7},{7,8},{8,9},{9,10},{10,1... | collective-permute-start | bytes 1228808 | tf_op jit(solution)/vmap(transpose(jvp()))/dot_general | solution.py:20
  (183 other events, 2706.2 us)
Sparse Core Ops, SparseCore 0:
  741.6 92.4 all-gather.13
  893.7 87.9 all-gather.11
  1052.6 66.1 all-gather.9
where the time goes:
time: 1150 us; the launch traced here: 1140 us
  matrix products  326 us (28%)
  waiting for transfers between devices  290 us (25%)
  starting transfers between devices  228 us (20%)
  other arithmetic  152 us (13%)
  local copies, waits for them, and re-layouts  81.9 us (7%)
  loops' own time  46.2 us (4%)
  between operations  15.3 us (1%)
    dot_general x19, matrix products, layer(): gate = jnp.dot(a, w['w_gate'], preferred_element_type=jnp.float32)  119 us
    dot_general x19, matrix products, layer(): up = jnp.dot(a, w['w_up'], preferred_element_type=jnp.float32)  113 us
    dot_general x34, waiting for transfers between devices, layer(): gate = jnp.dot(a, w['w_gate'], preferred_element_type=jnp.float32)  105 us
    dot_general x19, matrix products, matmul(): jnp.dot(a, w, preferred_element_type=jnp.float32).astype(jnp.bfloat16)  94.3 us
    dot_general x34, starting transfers between devices, layer(): gate = jnp.dot(a, w['w_gate'], preferred_element_type=jnp.float32)  83 us
    dot_general x34, starting transfers between devices, matmul(): jnp.dot(a, w, preferred_element_type=jnp.float32).astype(jnp.bfloat16)  73.3 us
    dot_general x34, waiting for transfers between devices, matmul(): jnp.dot(a, w, preferred_element_type=jnp.float32).astype(jnp.bfloat16)  71.6 us
    dot_general x34, starting transfers between devices, layer(): up = jnp.dot(a, w['w_up'], preferred_element_type=jnp.float32)  71.4 us
  transfers between devices with their start and end apart: 105, of which 49 were waited for; matrix products, arithmetic and copies ran while one was open for 32% of the time, Pallas kernels for 0%

commit v1 on v0

v1 whole, which is shorter than its diff:
```python
import jax
import jax.numpy as jnp
from jax import lax
from jax.experimental import pallas as pl
from jax.experimental.pallas import tpu as pltpu
from jax.sharding import PartitionSpec as P

F32, BF16 = jnp.float32, jnp.bfloat16
NT = (((1,), (1,)), ((), ()))


def dot(a, b):
    return jnp.dot(a, b, preferred_element_type=F32)


def dot_t(a, b):
    return lax.dot_general(a, b, NT, preferred_element_type=F32)


def sigmoid(x):
    return 0.5 * jnp.tanh(0.5 * x) + 0.5


def norm_scale(h):
    wide = h.astype(F32)
    return wide, lax.rsqrt(jnp.mean(wide * wide, -1, keepdims=True) + 1e-6)


def chain_kernel(x_ref, dy_ref, wg_hbm, wu_hbm, wd_hbm, act2_ref, dg2_ref, du2_ref, act1_ref, dg1_ref, du1_ref, at1_ref, at2_ref, dyt_ref, dht_ref,
                 wg, wu, wd, gate1, up1, sems, *, ft):
    ff = wg.shape[2]
    i = pl.program_id(0)
    copies = [pltpu.make_async_copy(src.at[l], dst.at[l], sems.at[l, k]) for l in range(2) for k, (src, dst) in enumerate(((wg_hbm, wg), (wu_hbm, wu), (wd_hbm, wd)))]

    @pl.when(i == 0)
    def _():
        for c in copies:
            c.start()

    def arrived(n):
        @pl.when(i == 0)
        def _():
            copies[n].wait()

    x = x_ref[...]
    dy = dy_ref[...]
    wide, s = norm_scale(x)
    a = (wide * s).astype(BF16)
    at1_ref[...] = a.T
    dyt_ref[...] = dy.T
    arrived(0)
    arrived(1)
    arrived(2)
    total = jnp.zeros(x.shape, F32)
    for f in range(0, ff, ft):
        fs = pl.ds(f, ft)
        gate = dot(a, wg[0, :, fs])
        up = dot(a, wu[0, :, fs])
        gate1[:, fs] = gate
        up1[:, fs] = up
        act = (gate * sigmoid(gate) * up).astype(BF16)
        act1_ref[:, fs] = act
        total += dot(act, wd[0, fs, :])
    h = x + total.astype(BF16)
    arrived(3)
    arrived(4)
    arrived(5)
    wide, s = norm_scale(h)
    a = (wide * s).astype(BF16)
    at2_ref[...] = a.T
    dag = jnp.zeros(x.shape, F32)
    dau = jnp.zeros(x.shape, F32)

    def back(dout, gate, up, l, fs, refs):
        dact = dot_t(dout, wd[l, fs, :]).astype(BF16).astype(F32)
        sig = sigmoid(gate)
        silu = gate * sig
        du = (dact * silu).astype(BF16)
        dg = (dact * up * (sig + silu * (1.0 - sig))).astype(BF16)
        refs[0][:, fs] = dg
        refs[1][:, fs] = du
        return dg, du, silu

    for f in range(0, ff, ft):
        fs = pl.ds(f, ft)
        gate = dot(a, wg[1, :, fs])
        up = dot(a, wu[1, :, fs])
        dg, du, silu = back(dy, gate, up, 1, fs, (dg2_ref, du2_ref))
        act2_ref[:, fs] = (silu * up).astype(BF16)
        dag += dot_t(dg, wg[1, :, fs])
        dau += dot_t(du, wu[1, :, fs])
    da = (dag.astype(BF16) + dau.astype(BF16)).astype(F32)
    inner = jnp.mean(da * wide, -1, keepdims=True)
    dh = dy + (da * s - wide * (s * s * s * inner)).astype(BF16)
    dht_ref[...] = dh.T
    for f in range(0, ff, ft):
        fs = pl.ds(f, ft)
        back(dh, gate1[:, fs], up1[:, fs], 0, fs, (dg1_ref, du1_ref))


def chain(x, dy, wg, wu, wd, tile=256, ft=1280):
    tokens, d = x.shape
    ff = wg.shape[2]
    rows = pl.BlockSpec((tile, d), lambda i: (i, 0))
    cols = pl.BlockSpec((d, tile), lambda i: (0, i))
    wide = pl.BlockSpec((tile, ff), lambda i: (i, 0))
    hbm = pl.BlockSpec(memory_space=pl.ANY)
    return pl.pallas_call(
        lambda *r: chain_kernel(*r, ft=ft),
        grid=(tokens // tile,),
        in_specs=[rows, rows, hbm, hbm, hbm],
        out_specs=[wide] * 6 + [cols] * 4,
        out_shape=[jax.ShapeDtypeStruct((tokens, ff), BF16)] * 6 + [jax.ShapeDtypeStruct((d, tokens), BF16)] * 4,
        scratch_shapes=[pltpu.VMEM(wg.shape, BF16), pltpu.VMEM(wu.shape, BF16), pltpu.VMEM(wd.shape, BF16), pltpu.VMEM((tile, ff), F32), pltpu.VMEM((tile, ff), F32), pltpu.SemaphoreType.DMA((2, 3))],
        compiler_params=pltpu.CompilerParams(dimension_semantics=("arbitrary",), vmem_limit_bytes=63 * 2**20),
        cost_estimate=pl.CostEstimate(flops=9 * 2 * tokens * d * ff, bytes_accessed=100 * 2**20, transcendentals=0),
    )(x, dy, wg, wu, wd)
MESH = pl.DeviceIdType.MESH
CHUNKS = (("down", 1), ("gate", 1), ("up", 1), ("down", 0), ("gate", 0), ("up", 0))
FT = 512
PERIOD, STEP, TILE = 25.0, 5.0, 1.7


def adamw(w, m, v, g):
    m = 0.9 * m + 0.1 * g
    v = 0.95 * v + 0.05 * g * g
    step = m * lax.rsqrt(v + 1e-8) + 0.1 * w
    return (w - 0.02 * step).astype(BF16), m, v


class Chunk:
    def __init__(self, place, bufs, own, ssem, rsem, free):
        self.__dict__.update(place)
        (self.T, self.D, self.YA, self.EA, self.FA, self.EB, self.FB, self.YB) = bufs
        self.w, self.m, self.v = own
        self.ssem, self.rsem, self.free = ssem, rsem, free
        self.R = self.T.shape[3]
        self.RA = self.R * 3 // 5
        self.A, self.B = pl.ds(0, self.RA), pl.ds(self.RA, self.R - self.RA)
        self.sent = []

    def copy(self, src, dst, s, r, dev):
        return pltpu.make_async_remote_copy(src_ref=src, dst_ref=dst, send_sem=self.ssem.at[s], recv_sem=self.rsem.at[r], device_id=dev, device_id_type=MESH)

    def send(self, cond, src, dst, s, r, dev):
        base, o = s if isinstance(s, tuple) else (s, None)
        self.copy(src, dst, base if o is None else base + o, r, dev).start()
        self.sent.append((cond, src.shape, base, o))

    def wait_sent(self):
        R, RA = self.R, self.RA
        like = {
            (2, 4, R): lambda: self.D,
            (RA,): lambda: self.YA.at[0],
            (R - RA,): lambda: self.YB,
            (2, R - RA): lambda: self.EB.at[0],
        }
        for cond, shape, base, o in self.sent[1:]:
            def wait():
                ref = like[tuple(shape[:-1])]()
                self.copy(ref, ref, base if o is None else base + o, 0, self.partner).wait_send()

            self.when(cond, wait)

    def got(self, dst, r):
        self.copy(dst, dst, 0, r, self.partner).wait_recv()

    def when(self, cond, f):
        if cond is None:
            f()
        else:
            pl.when(cond)(f)

    def add(self, dst, *srcs):
        dst[...] = sum(s[...].astype(F32) for s in (dst, *srcs)).astype(BF16)

    def own_y(self, o, rows):
        return self.T.at[self.y, o, self.c, rows, :]

    def both(self, o):
        return self.T.at[:, o, self.c, self.B, :]

    def s0(self):
        self.send(None, self.T.at[:, :, 1 - self.c], self.D, 0, 0, self.partner)

    def s1(self):
        self.got(self.D, 0)
        for n, o in enumerate((self.e1, self.i1, self.i0, self.e0)):
            t = self.D.at[1 - self.y, o, self.A, :]
            self.add(t, self.T.at[1 - self.y, o, self.c, self.A, :])
            self.send(None, t, self.YA.at[o], (1, o), 1 + o, self.across)

        def end():
            for slot, o in enumerate((self.e1, self.i1, self.i0)):
                t = self.D.at[:, o, self.B, :]
                self.add(t, self.both(o))
                self.send(self.end, t, self.EB.at[slot], 11 + slot, 11 + slot, self.inner)

        self.when(self.end, end)

    def s2(self):
        self.copy(self.D, self.D, 0, 0, self.partner).wait_send()
        pl.semaphore_signal(self.free, inc=1, device_id=self.partner, device_id_type=MESH)

        def mid():
            for slot, o in enumerate((self.e1, self.i1)):
                self.got(self.EB.at[slot], 11 + slot)
                t = self.D.at[:, o, self.B, :]
                self.add(t, self.both(o), self.EB.at[slot])
                self.send(self.mid, t, self.FB.at[slot], 14 + slot, 14 + slot, self.inner)

        self.when(self.mid, mid)

    def got_y(self, o):
        self.got(self.YA.at[o], 1 + o)

    def s3(self):
        def end():
            for slot, o in enumerate((self.e1, self.i1, self.i0)):
                self.got_y(o)
                t = self.YA.at[o]
                self.add(t, self.own_y(o, self.A), self.D.at[self.y, o, self.A, :])
                self.send(self.end, t, self.EA.at[slot], 5 + slot, 5 + slot, self.inner)

        def mid():
            self.got(self.FB.at[0], 14)
            t = self.D.at[:, self.e0, self.B, :]
            self.add(t, self.both(self.e0), self.FB.at[0])
            self.send(self.mid, t, self.FB.at[1], 16, 16, self.outer)

        self.when(self.end, end)
        self.when(self.mid, mid)

    def s4(self):
        def mid():
            for slot, o in enumerate((self.e1, self.i1)):
                self.got(self.EA.at[slot], 5 + slot)
                self.got_y(o)
                t = self.YA.at[o]
                self.add(t, self.own_y(o, self.A), self.D.at[self.y, o, self.A, :], self.EA.at[slot])
                self.send(self.mid, t, self.FA.at[slot], 8 + slot, 8 + slot, self.inner)

        self.when(self.mid, mid)
        own = self.T.at[1 - self.y, self.z, self.c, self.B, :]
        d = self.D.at[1 - self.y, self.z, self.B, :]
        t = self.FB.at[1, 1 - self.y]

        def mid2():
            self.got(self.FB.at[1], 15)
            self.got(self.EB.at[2], 13)
            self.add(t, own, d, self.EB.at[2, 1 - self.y])

        def end2():
            self.got(self.FB.at[1], 16)
            self.add(t, own, d)

        self.when(self.mid, mid2)
        self.when(self.end, end2)
        self.send(None, t, self.YB, 17, 17, self.across)

    def step(self, rows, *srcs):
        t = self.own_y(self.z, rows)
        g = sum(s[...].astype(F32) for s in (t, *srcs)).astype(BF16).astype(F32)
        w, m, v = adamw(self.w[rows, :].astype(F32), self.m[rows, :], self.v[rows, :], g)
        t[...] = w
        self.m[rows, :] = m
        self.v[rows, :] = v

    def s5(self):
        def mid():
            self.got(self.FA.at[0], 8)
            self.got_y(self.e0)
            t = self.YA.at[self.e0]
            self.add(t, self.own_y(self.e0, self.A), self.D.at[self.y, self.e0, self.A, :], self.FA.at[0])
            self.send(self.mid, t, self.FA.at[1], 10, 10, self.outer)

        self.when(self.mid, mid)
        self.got(self.YB, 17)
        d = self.D.at[self.y, self.z, self.B, :]
        self.when(self.mid, lambda: self.step(self.B, d, self.YB, self.FB.at[1, self.y], self.EB.at[2, self.y]))
        self.when(self.end, lambda: self.step(self.B, d, self.YB, self.FB.at[1, self.y]))
        t = self.own_y(self.z, self.B)
        self.send(None, t, t, 30, 30, self.across)

    def s6(self):
        self.got_y(self.z)
        d = self.D.at[self.y, self.z, self.A, :]

        def mid():
            self.got(self.FA.at[1], 9)
            self.got(self.EA.at[2], 7)
            self.step(self.A, d, self.YA.at[self.z], self.FA.at[1], self.EA.at[2])

        def end():
            self.got(self.FA.at[1], 10)
            self.step(self.A, d, self.YA.at[self.z], self.FA.at[1])

        self.when(self.mid, mid)
        self.when(self.end, end)
        self.give_a(self.z, None, self.mid, None)
        self.got(self.T.at[1 - self.y, self.z, self.c, self.B, :], 30)
        self.give_b(self.z, None, self.mid)

    def give_a(self, o, inward, outward, cond):
        t = self.own_y(o, self.A)
        if inward is not False:
            self.when(inward, lambda: self.send(inward, t, t, (18, o), 18 + o, self.inner))
        if outward is not False:
            self.when(outward, lambda: self.send(outward, t, t, (22, o), 18 + o, self.outer))
        self.send(cond, t, t, (26, o), 26 + o, self.across)

    def give_b(self, o, inward, outward):
        t = self.both(o)
        if inward is not False:
            self.when(inward, lambda: self.send(inward, t, t, (31, o), 31 + o, self.inner))
        if outward is not False:
            self.when(outward, lambda: self.send(outward, t, t, (35, o), 31 + o, self.outer))

    def got_a(self, o):
        self.got(self.own_y(o, self.A), 18 + o)

    def got_b(self, o):
        self.got(self.both(o), 31 + o)

    def plain(self, cond, o, inward, outward, which):
        if which == "a":
            t = self.own_y(o, self.A)
            self.got_a(o)
            base = 18
        else:
            t = self.both(o)
            self.got_b(o)
            base = 31
        if inward:
            self.send(cond, t, t, (base, o), base + o, self.inner)
        if outward:
            self.send(cond, t, t, (base + 4, o), base + o, self.outer)
        if which == "a":
            self.send(cond, t, t, (26, o), 26 + o, self.across)

    def g1(self, which):
        def mid():
            self.plain(self.mid, self.e0, True, False, which)
            self.plain(self.mid, self.i1, False, True, which)

        self.when(self.mid, mid)
        self.when(self.end, lambda: self.plain(self.end, self.i0, False, False, which))

    def g2(self, which):
        self.when(self.mid, lambda: self.plain(self.mid, self.e1, False, True, which))
        self.when(self.end, lambda: self.plain(self.end, self.i1, False, False, which))

    def g3(self, which):
        self.when(self.end, lambda: self.plain(self.end, self.e1, False, False, which))

    def s7(self):
        self.g1("a")

    def s8(self):
        self.g1("b")
        self.g2("a")

    def s9(self):
        self.g2("b")
        self.g3("a")

    def s10(self):
        self.g3("b")
        for o in range(4):
            self.got(self.T.at[1 - self.y, o, self.c, self.A, :], 26 + o)
        pl.semaphore_wait(self.free, 1)
        t = self.T.at[:, :, self.c]
        self.send(None, t, t, 39, 39, self.partner)

    def s11(self):
        self.got(self.T.at[:, :, 1 - self.c], 39)
        self.wait_sent()

    STEPS = ("s0", "s1", "s2", "s3", "s4", "s5", "s6", "s7", "s8", "s9", "s10", "s11")


def kernel(act2, dg2, du2, act1, dg1, du1, at1, at2, dyt, dht, wg, wu, wd, mg, mu, md, vg, vu, vd,
           o_wg, o_wu, o_wd, o_mg, o_mu, o_md, o_vg, o_vu, o_vd,
           tg, tu, td, dG, dDn, yaG, yaD, eaG, eaD, faG, faD, ebG, ebD, fbG, fbD, ybG, ybD,
           lhs, rhs, sw_g, sw_u, sw_d, sm_g, sm_u, sm_d, sv_g, sv_u, sv_d,
           ssem, rsem, lsem, tsem, isem, osem, free):
    rep, me = lax.axis_index("rep"), lax.axis_index("dp")
    c, z, y = me % 2, (me // 2) % 4, me // 8

    def dev(y, z, c):
        return (rep, y * 8 + z * 2 + c)

    low = z < 2
    e0, i0, i1, e1 = (jnp.where(low, p, 3 - p) for p in range(4))
    end = (z == 0) | (z == 3)
    mid = (z == 1) | (z == 2)
    inner = dev(y, jnp.where(end, i0, i1), c)
    outer = dev(y, e0, c)
    place = dict(y=y, z=z, c=c, e0=e0, i0=i0, i1=i1, e1=e1, end=end, mid=mid, inner=inner, outer=outer, across=dev(1 - y, z, c), partner=dev(y, z, 1 - c))

    owns = {"gate": (sw_g, sm_g, sv_g), "up": (sw_u, sm_u, sv_u), "down": (sw_d, sm_d, sv_d)}
    T = {"gate": tg, "up": tu, "down": td}
    loads, stores = [], []
    for n, (name, hw, hm, hv, ow, om, ov) in enumerate((("gate", wg, mg, vg, o_wg, o_mg, o_vg), ("up", wu, mu, vu, o_wu, o_mu, o_vu), ("down", wd, md, vd, o_wd, o_md, o_vd))):
        sw, sm, sv = owns[name]
        loads += [pltpu.make_async_copy(hw.at[:, me], sw, isem.at[n, 0]), pltpu.make_async_copy(hm, sm, isem.at[n, 1]), pltpu.make_async_copy(hv, sv, isem.at[n, 2])]
    outs = {"gate": (o_wg, o_mg, o_vg), "up": (o_wu, o_mu, o_vu), "down": (o_wd, o_md, o_vd)}

    left = {("down", 1): dyt, ("gate", 1): at2, ("up", 1): at2, ("down", 0): dht, ("gate", 0): at1, ("up", 0): at1}
    right = {("down", 1): act2, ("gate", 1): dg2, ("up", 1): du2, ("down", 0): act1, ("gate", 0): dg1, ("up", 0): du1}
    tiles = right[CHUNKS[0]].shape[1] // FT

    def rhs_copy(k, j):
        t = tiles * k + j
        return pltpu.make_async_copy(right[CHUNKS[k]].at[:, pl.ds(j * FT, FT)], rhs.at[t % 2], tsem.at[t % 2])

    def lhs_copy(k):
        s = 0 if CHUNKS[k][0] == "down" else 1
        return pltpu.make_async_copy(left[CHUNKS[k]], lhs.at[s], lsem.at[s])

    lhs_copy(0).start()
    rhs_copy(0, 0).start()
    lhs_copy(1).start()

    barrier = pltpu.get_barrier_semaphore()
    for d, cond in ((place["partner"], None), (place["across"], None), (inner, None), (outer, mid)):
        if cond is None:
            pl.semaphore_signal(barrier, inc=1, device_id=d, device_id_type=MESH)
        else:
            @pl.when(cond)
            def _():
                pl.semaphore_signal(barrier, inc=1, device_id=d, device_id_type=MESH)
    pl.when(mid)(lambda: pl.semaphore_wait(barrier, 4))
    pl.when(end)(lambda: pl.semaphore_wait(barrier, 3))

    chunks = []
    counts = {"gate": 0, "down": 0}
    for k, (name, l) in enumerate(CHUNKS):
        kind = "down" if name == "down" else "gate"
        n = counts[kind]
        counts[kind] += 1
        pick = 1 if kind == "down" else 0
        bufs = [T[name].at[l]] + [b[pick].at[n] for b in ((dG, dDn), (yaG, yaD), (eaG, eaD), (faG, faD), (ebG, ebD), (fbG, fbD), (ybG, ybD))]
        chunks.append(Chunk(place, bufs, [b.at[l] for b in owns[name]], ssem.at[k], rsem.at[k], free.at[k]))

    def finish(k):
        name, l = CHUNKS[k]
        for i, (src, dst) in enumerate(zip((T[name],) + owns[name][1:], outs[name])):
            cp = pltpu.make_async_copy(src.at[l], dst.at[l], osem.at[k, i])
            cp.start()
            stores.append(cp)

    started = set()

    def run(k, s):
        if (k, s) == (0, 5):
            for cp in loads:
                cp.wait()
        getattr(chunks[k], Chunk.STEPS[s])()
        if s == len(Chunk.STEPS) - 1:
            finish(k)

    plan = sorted((max(tiles * (k + 1), tiles + (PERIOD * k + STEP * s) / TILE), s * -1, k, s) for k in range(len(CHUNKS)) for s in range(len(Chunk.STEPS)))
    total_tiles = tiles * len(CHUNKS)
    slots = {}
    for at, _, k, s in plan:
        slots.setdefault(min(int(at), total_tiles), []).append((k, s))
    for v in slots.values():
        pass

    for k, (name, l) in enumerate(CHUNKS):
        if k == 0:
            for cp in loads:
                cp.start()
        if k in (0, 1, 3, 4):
            lhs_copy(k).wait()
        side = 0 if name == "down" else 1

        def tile(j, _, k=k, name=name, l=l, side=side):
            t = tiles * k + j
            rhs_copy(k, j).wait()

            @pl.when(j < tiles - 1)
            def _():
                rhs_copy(k, j + 1).start()

            if k + 1 < len(CHUNKS):
                @pl.when(j == tiles - 1)
                def _():
                    rhs_copy(k + 1, 0).start()

            out = jnp.dot(lhs[side], rhs[t % 2], preferred_element_type=F32).astype(BF16)
            if name == "down":
                out = out.T
                for q in range(FT // 32):
                    n = (FT // 32) * j + q
                    b, r = n // 5, pl.multiple_of((n % 5) * 32, 32)
                    td[l, b // 8, (b // 2) % 4, b % 2, pl.ds(r, 32), :] = out[32 * q : 32 * q + 32]
            else:
                T[name][l, :, :, :, :, pl.ds(pl.multiple_of(j * FT, FT), FT)] = out.reshape(2, 4, 2, 40, FT)
            for jj in range(tiles):
                todo = slots.get(tiles * k + jj, [])
                if todo:
                    @pl.when(j == jj)
                    def _(todo=todo):
                        for kk, s in todo:
                            run(kk, s)
            return 0

        lax.fori_loop(0, tiles, tile, 0)
        if k == 0:
            lhs_copy(3).start()
        if k == 2:
            lhs_copy(4).start()
    for kk, s in slots.get(total_tiles, []):
        run(kk, s)
    for cp in stores:
        cp.wait()


def comm(parts, weights, moments, ):
    hbm = pl.BlockSpec(memory_space=pl.ANY)
    wg, wu, wd = weights
    blocks = [w.reshape(w.shape[0], 16, w.shape[1] // 16, w.shape[2]) for w in weights]
    outs = [jax.ShapeDtypeStruct((2, 2, 4, 2) + b.shape[2:], BF16) for b in blocks]
    outs += [jax.ShapeDtypeStruct(t.shape, F32) for t in moments]
    g, d = (40, 2560), (160, 640)

    def pair(*lead, a=None):
        def rows(s):
            return {None: s[0], "A": s[0] * 3 // 5, "B": s[0] * 2 // 5}[a]
        return [pltpu.VMEM((4, *lead, rows(g), g[1]), BF16), pltpu.VMEM((2, *lead, rows(d), d[1]), BF16)]

    scratch = [pltpu.VMEM((2, 2, 4, 2) + b.shape[2:], BF16) for b in blocks]
    scratch += pair(2, 4) + pair(4, a="A") + pair(3, a="A") + pair(2, a="A") + pair(3, 2, a="B") + pair(2, 2, a="B") + pair(a="B")
    scratch += [pltpu.VMEM((2, 640, 2048), BF16), pltpu.VMEM((2, 2048, FT), BF16)]
    scratch += [pltpu.VMEM((2,) + b.shape[2:], BF16) for b in blocks]
    scratch += [pltpu.VMEM((2,) + b.shape[2:], F32) for b in blocks] * 2
    dma = pltpu.SemaphoreType.DMA
    scratch += [dma((6, 40)), dma((6, 40)), dma((2,)), dma((2,)), dma((3, 3)), dma((6, 3)), pltpu.SemaphoreType.REGULAR((6,))]
    return pl.pallas_call(
        kernel,
        in_specs=[hbm] * 19,
        out_specs=[hbm] * 9,
        out_shape=outs,
        scratch_shapes=scratch,
        compiler_params=pltpu.CompilerParams(collective_id=0, has_side_effects=True, vmem_limit_bytes=67043328),
        cost_estimate=pl.CostEstimate(flops=6 * 2 * 2048 * 640 * 2560, bytes_accessed=100 * 2**20, transcendentals=0),
    )(*parts, *blocks, *moments)


def solution(mesh):
    def step(x, dy, wg, wu, wd, *moments):
        parts = chain(x[0], dy[0], wg, wu, wd)
        new = comm(parts, (wg, wu, wd), moments)
        return tuple(t.reshape(w.shape) for t, w in zip(new, (wg, wu, wd))) + tuple(new[3:])

    whole, rows = P(None, None, None), P(None, "dp", None)
    return jax.shard_map(
        step,
        mesh=mesh,
        in_specs=(P(("rep", "dp")),) * 2 + (whole,) * 3 + (rows,) * 6,
        out_specs=(P("rep", None, None),) * 3 + (P("rep", "dp", None),) * 6,
        check_vma=False,
    )
```

time: 1150 us -> 371 us (0.32)
  Pallas kernels: 0 us -> 350 us
  matrix products: 326 us -> 0 us
  waiting for transfers between devices: 290 us -> 0 us
  starting transfers between devices: 228 us -> 0 us
  other arithmetic: 152 us -> 0.01 us
  local copies, waits for them, and re-layouts: 81.9 us -> 20.2 us
  loops' own time: 46.2 us -> 0 us
  between operations: 15.3 us -> 0.69 us
    pallas_call x0 -> x2, Pallas kernels: none -> 350 us  [the longest x1 255 us: comm(): pl.pallas_call(kernel, in_specs=[hbm] * 19, out_specs=[hbm] * 9, out_shap...]
    dot_general x57 -> x0, matrix products: 326 us -> none  [the longest x19 119 us: layer(): gate = jnp.dot(a, w['w_gate'], preferred_element_type=jnp.float32)]
    dot_general x102 -> x0, starting transfers between devices: 228 us -> none  [the longest x34 83 us: layer(): gate = jnp.dot(a, w['w_gate'], preferred_element_type=jnp.float32)]
    dot_general x102 -> x0, waiting for transfers between devices: 224 us -> none  [the longest x34 105 us: layer(): gate = jnp.dot(a, w['w_gate'], preferred_element_type=jnp.float32)]
    dot_general x112 -> x0, other arithmetic: 107 us -> none
    reshape x3 -> x0, waiting for transfers between devices: 66.3 us -> none  [step(): t.reshape(-1, *t.shape[2:])]
    another operation x6 -> x0, loops' own time: 46.2 us -> none  [the longest x2 16 us: layer(): up = jnp.dot(a, w['w_up'], preferred_element_type=jnp.float32)]
    unnamed x69 -> x27, local copies, waits for them, and re-layouts: 60.9 us -> 20.2 us
  transfers between devices with their start and end apart: 105 -> 0, of which waited for: 49 -> 0; matrix products, arithmetic and copies ran while one was open for 32% -> 0% of each run, Pallas kernels for 0% -> 0%
where the time goes in v1:
time: 371 us; the launch traced here: 370 us
  Pallas kernels  350 us (94%)
  local copies, waits for them, and re-layouts  20.2 us (5%)
    pallas_call x1, Pallas kernels, comm(): pl.pallas_call(kernel, in_specs=[hbm] * 19, out_specs=[hbm] * 9, out_shap...  255 us
    pallas_call x1, Pallas kernels, chain(): pl.pallas_call(lambda *r: chain_kernel(*r, ft=ft), grid=(tokens // tile,)...  94.9 us
    unnamed x27, local copies, waits for them, and re-layouts  20.2 us

profile of v1, /device:TPU:0, one launch (start us, length us, event | category | flops | bytes accessed | tf_op | source)
XLA Modules:
  0.0 370.5 jit_solution(256290393186307859)
XLA Ops:
  0.6 94.9 %shard_map.178 = (bf16[2048,2560]{1,0:T(8,128)(2,1)}, bf16[2048,2560]{1,0:T(8,128)(2,1)}, bf16[2048,2560]{1,0:T(8,128)(2,1)}, bf16[2048,2560]{1,0:T(8,128)(2,1)}...) custom-call(bf16[2048,640]{1,0:T(8,128)(2,1)} %bitcast.16, ...), custom_call_target="tpu_custom_call" | custom-call | flops 60397977600 | bytes 104857600 | tf_op jit(solution)/shard_map/pallas_call | solution.py:108
  95.6 254.7 %shard_map.179 = (bf16[2,2,4,2,40,2560]{5,4,3,2,1,0:T(8,128)(2,1)}, bf16[2,2,4,2,40,2560]{5,4,3,2,1,0:T(8,128)(2,1)}, bf16[2,2,4,2,160,640]{5,4,3,2,1,0:T(8,128)...) custom-call(bf16[2048,2560]{1,0:T(8,128)(2,1)} %get-tuple-element.28, ...), custom_call_target="tpu_custom_call" | custom-call | flops 40265318400 | bytes 104857600 | tf_op jit(solution)/shard_map/pallas_call | solution.py:541
  350.3 0.0 copy-start
  350.3 0.0 slice-start
  350.3 6.8 %copy.29 = bf16[2,640,2560]{2,1,0:T(8,128)(2,1)} copy(bf16[2,640,2560]{2,1,0:T(8,128)(2,1)} %bitcast.12) | data formatting | bytes 13107200
  357.1 0.0 copy-done
  357.1 0.0 slice-start.1
  357.1 3.3 copy.30
  360.4 0.0 slice-done
  360.4 1.4 slice-done.1
  361.8 0.0 copy-start.5
  361.8 3.3 copy.31
  365.1 0.0 copy-done.6
  365.1 0.9 copy.32
  366.0 0.0 copy-done.5
  366.0 0.9 copy.33
  366.9 0.0 copy-done.4
  366.9 0.9 copy.34
  367.8 0.0 copy-done.3
  367.8 0.9 copy.35
  368.7 0.0 copy-done.2
  368.7 0.9 copy.36
  369.6 0.0 copy-done.1
  369.6 0.9 copy.37
  (6 shorter events, 0.0 us)
Async XLA Ops:
  350.3 6.8 %copy-start = (bf16[2,2,4,2,40,2560]{5,4,3,2,1,0:T(8,128)(2,1)S(1)}, bf16[2,2,4,2,40,2560]{5,4,3,2,1,0:T(8,128)(2,1)}, u32[]{:S(2)}) copy-start(bf16[2,2,4,2,40,2560]{5,4,3,2,1,0:T(8,128)(2,1)} %get-tuple-element.39) | copy-start | bytes 19660804
  350.3 10.1 %slice-start = ((s8[6553600]{0:T(1024)(128)(4,1)}), s8[4194304]{0:T(1024)(128)(4,1)S(1)}, s32[]{:S(2)}) async-start(s8[6553600]{0:T(1024)(128)(4,1)} %bitcast.8), calls=%async_computation | async-start | bytes 8388608
  357.1 4.7 %slice-start.1 = ((s8[6553600]{0:T(1024)(128)(4,1)}), s8[2359296]{0:T(1024)(128)(4,1)S(1)}, s32[]{:S(2)}) async-start(s8[6553600]{0:T(1024)(128)(4,1)} %bitcast.8), calls=%async_computation.1 | async-start | bytes 4718592
  361.8 3.3 copy-start.6
  361.8 4.2 %copy-start.5 = (f32[2,40,2560]{2,1,0:T(8,128)S(1)}, f32[2,40,2560]{2,1,0:T(8,128)}, u32[]{:S(2)}) copy-start(f32[2,40,2560]{2,1,0:T(8,128)} %get-tuple-element.60) | copy-start | bytes 2457604
  361.8 5.1 %copy-start.4 = (f32[2,160,640]{2,1,0:T(8,128)S(1)}, f32[2,160,640]{2,1,0:T(8,128)}, u32[]{:S(2)}) copy-start(f32[2,160,640]{2,1,0:T(8,128)} %get-tuple-element.61) | copy-start | bytes 2457604
  361.8 6.0 %copy-start.3 = (f32[2,40,2560]{2,1,0:T(8,128)S(1)}, f32[2,40,2560]{2,1,0:T(8,128)}, u32[]{:S(2)}) copy-start(f32[2,40,2560]{2,1,0:T(8,128)} %get-tuple-element.62) | copy-start | bytes 2457604
  365.1 3.6 copy-start.2
  365.1 4.5 %copy-start.1 = (f32[2,160,640]{2,1,0:T(8,128)S(1)}, f32[2,160,640]{2,1,0:T(8,128)}, u32[]{:S(2)}) copy-start(f32[2,160,640]{2,1,0:T(8,128)} %get-tuple-element.64) | copy-start | bytes 2457604

commit v2 on v1

--- a/solution.py
+++ b/solution.py
@@ -50,7 +50,6 @@
     dyt_ref[...] = dy.T
     arrived(0)
     arrived(1)
-    arrived(2)
     total = jnp.zeros(x.shape, F32)
     for f in range(0, ff, ft):
         fs = pl.ds(f, ft)
@@ -60,6 +59,8 @@
         up1[:, fs] = up
         act = (gate * sigmoid(gate) * up).astype(BF16)
         act1_ref[:, fs] = act
+        if f == 0:
+            arrived(2)
         total += dot(act, wd[0, fs, :])
     h = x + total.astype(BF16)
     arrived(3)
@@ -116,9 +117,10 @@
         cost_estimate=pl.CostEstimate(flops=9 * 2 * tokens * d * ff, bytes_accessed=100 * 2**20, transcendentals=0),
     )(x, dy, wg, wu, wd)
 MESH = pl.DeviceIdType.MESH
-CHUNKS = (("down", 1), ("gate", 1), ("up", 1), ("down", 0), ("gate", 0), ("up", 0))
+CHUNKS = (("gate", 1), ("up", 1), ("down", 1), ("gate", 0), ("up", 0), ("down", 0))
 FT = 512
-PERIOD, STEP, TILE = 25.0, 5.0, 1.7
+SPLIT = (1, 1, 1, 1, 1, 2)
+PERIOD, STEP, TILE = 14.0, 4.0, 1.7
 
 
 def adamw(w, m, v, g):
@@ -380,10 +382,10 @@
 
 
 def kernel(act2, dg2, du2, act1, dg1, du1, at1, at2, dyt, dht, wg, wu, wd, mg, mu, md, vg, vu, vd,
-           o_wg, o_wu, o_wd, o_mg, o_mu, o_md, o_vg, o_vu, o_vd,
-           tg, tu, td, dG, dDn, yaG, yaD, eaG, eaD, faG, faD, ebG, ebD, fbG, fbD, ybG, ybD,
-           lhs, rhs, sw_g, sw_u, sw_d, sm_g, sm_u, sm_d, sv_g, sv_u, sv_d,
-           ssem, rsem, lsem, tsem, isem, osem, free):
+           tg, tu, td, sm_g, sm_u, sm_d, sv_g, sv_u, sv_d,
+           dG, dDn, yaG, yaD, eaG, eaD, faG, faD, ebG, ebD, fbG, fbD, ybG, ybD,
+           lhs, rhs, sw_g, sw_u, sw_d,
+           ssem, rsem, lsem, tsem, isem, free):
     rep, me = lax.axis_index("rep"), lax.axis_index("dp")
     c, z, y = me % 2, (me // 2) % 4, me // 8
 
@@ -400,11 +402,10 @@
 
     owns = {"gate": (sw_g, sm_g, sv_g), "up": (sw_u, sm_u, sv_u), "down": (sw_d, sm_d, sv_d)}
     T = {"gate": tg, "up": tu, "down": td}
-    loads, stores = [], []
-    for n, (name, hw, hm, hv, ow, om, ov) in enumerate((("gate", wg, mg, vg, o_wg, o_mg, o_vg), ("up", wu, mu, vu, o_wu, o_mu, o_vu), ("down", wd, md, vd, o_wd, o_md, o_vd))):
+    loads = []
+    for n, (name, hw, hm, hv) in enumerate((("gate", wg, mg, vg), ("up", wu, mu, vu), ("down", wd, md, vd))):
         sw, sm, sv = owns[name]
         loads += [pltpu.make_async_copy(hw.at[:, me], sw, isem.at[n, 0]), pltpu.make_async_copy(hm, sm, isem.at[n, 1]), pltpu.make_async_copy(hv, sv, isem.at[n, 2])]
-    outs = {"gate": (o_wg, o_mg, o_vg), "up": (o_wu, o_mu, o_vu), "down": (o_wd, o_md, o_vd)}
 
     left = {("down", 1): dyt, ("gate", 1): at2, ("up", 1): at2, ("down", 0): dht, ("gate", 0): at1, ("up", 0): at1}
     right = {("down", 1): act2, ("gate", 1): dg2, ("up", 1): du2, ("down", 0): act1, ("gate", 0): dg1, ("up", 0): du1}
@@ -420,7 +421,7 @@
 
     lhs_copy(0).start()
     rhs_copy(0, 0).start()
-    lhs_copy(1).start()
+    lhs_copy(2).start()
 
     barrier = pltpu.get_barrier_semaphore()
     for d, cond in ((place["partner"], None), (place["across"], None), (inner, None), (outer, mid)):
@@ -433,46 +434,48 @@
     pl.when(mid)(lambda: pl.semaphore_wait(barrier, 4))
     pl.when(end)(lambda: pl.semaphore_wait(barrier, 3))
 
-    chunks = []
-    counts = {"gate": 0, "down": 0}
+    def part(k, ref, h):
+        if SPLIT[k] == 1:
+            return ref
+        rows, cols = ref.shape[-2] // SPLIT[k], ref.shape[-1] // SPLIT[k]
+        lead = (slice(None),) * (len(ref.shape) - 2)
+        if CHUNKS[k][0] == "down":
+            return ref.at[lead + (pl.ds(h * rows, rows), slice(None))]
+        return ref.at[lead + (slice(None), pl.ds(h * cols, cols))]
+
+    chunks, which = [], []
+    counts = [0, 0]
     for k, (name, l) in enumerate(CHUNKS):
-        kind = "down" if name == "down" else "gate"
-        n = counts[kind]
-        counts[kind] += 1
-        pick = 1 if kind == "down" else 0
-        bufs = [T[name].at[l]] + [b[pick].at[n] for b in ((dG, dDn), (yaG, yaD), (eaG, eaD), (faG, faD), (ebG, ebD), (fbG, fbD), (ybG, ybD))]
-        chunks.append(Chunk(place, bufs, [b.at[l] for b in owns[name]], ssem.at[k], rsem.at[k], free.at[k]))
-
-    def finish(k):
-        name, l = CHUNKS[k]
-        for i, (src, dst) in enumerate(zip((T[name],) + owns[name][1:], outs[name])):
-            cp = pltpu.make_async_copy(src.at[l], dst.at[l], osem.at[k, i])
-            cp.start()
-            stores.append(cp)
-
-    started = set()
+        pick = 1 if name == "down" else 0
+        n = counts[pick]
+        counts[pick] += 1
+        for h in range(SPLIT[k]):
+            bufs = [T[name].at[l]] + [b[pick].at[n] for b in ((dG, dDn), (yaG, yaD), (eaG, eaD), (faG, faD), (ebG, ebD), (fbG, fbD), (ybG, ybD))]
+            i = len(chunks)
+            chunks.append(Chunk(place, [part(k, b, h) for b in bufs], [part(k, b.at[l], h) for b in owns[name]], ssem.at[i], rsem.at[i], free.at[i]))
+            which.append((k, h))
 
     def run(k, s):
         if (k, s) == (0, 5):
             for cp in loads:
                 cp.wait()
         getattr(chunks[k], Chunk.STEPS[s])()
-        if s == len(Chunk.STEPS) - 1:
-            finish(k)
-
-    plan = sorted((max(tiles * (k + 1), tiles + (PERIOD * k + STEP * s) / TILE), s * -1, k, s) for k in range(len(CHUNKS)) for s in range(len(Chunk.STEPS)))
+
+    def ready(i):
+        k, h = which[i]
+        return tiles * (k + 1) - 1 if CHUNKS[k][0] == "down" else tiles * k - (-tiles * (h + 1) // SPLIT[k]) - 1
+
+    plan = sorted((max(ready(i), ready(0) + (PERIOD * (which[i][0] + which[i][1] / SPLIT[which[i][0]]) + STEP * s) / TILE) + s * 1e-6, i, s) for i in range(len(chunks)) for s in range(len(Chunk.STEPS)))
     total_tiles = tiles * len(CHUNKS)
     slots = {}
-    for at, _, k, s in plan:
+    for at, k, s in plan:
         slots.setdefault(min(int(at), total_tiles), []).append((k, s))
-    for v in slots.values():
-        pass
 
     for k, (name, l) in enumerate(CHUNKS):
         if k == 0:
             for cp in loads:
                 cp.start()
-        if k in (0, 1, 3, 4):
+        if k in (0, 2, 3, 5):
             lhs_copy(k).wait()
         side = 0 if name == "down" else 1
 
@@ -508,22 +511,18 @@
             return 0
 
         lax.fori_loop(0, tiles, tile, 0)
-        if k == 0:
-            lhs_copy(3).start()
-        if k == 2:
-            lhs_copy(4).start()
+        if k in (1, 2):
+            lhs_copy(2 * k + 1).start()
     for kk, s in slots.get(total_tiles, []):
         run(kk, s)
-    for cp in stores:
-        cp.wait()
 
 
 def comm(parts, weights, moments, ):
     hbm = pl.BlockSpec(memory_space=pl.ANY)
     wg, wu, wd = weights
     blocks = [w.reshape(w.shape[0], 16, w.shape[1] // 16, w.shape[2]) for w in weights]
-    outs = [jax.ShapeDtypeStruct((2, 2, 4, 2) + b.shape[2:], BF16) for b in blocks]
-    outs += [jax.ShapeDtypeStruct(t.shape, F32) for t in moments]
+    outs = [pltpu.VMEM((2, 2, 4, 2) + b.shape[2:], BF16) for b in blocks]
+    outs += [pltpu.VMEM(t.shape, F32) for t in moments]
     g, d = (40, 2560), (160, 640)
 
     def pair(*lead, a=None):
@@ -531,28 +530,46 @@
             return {None: s[0], "A": s[0] * 3 // 5, "B": s[0] * 2 // 5}[a]
         return [pltpu.VMEM((4, *lead, rows(g), g[1]), BF16), pltpu.VMEM((2, *lead, rows(d), d[1]), BF16)]
 
-    scratch = [pltpu.VMEM((2, 2, 4, 2) + b.shape[2:], BF16) for b in blocks]
-    scratch += pair(2, 4) + pair(4, a="A") + pair(3, a="A") + pair(2, a="A") + pair(3, 2, a="B") + pair(2, 2, a="B") + pair(a="B")
+    scratch = pair(2, 4) + pair(4, a="A") + pair(3, a="A") + pair(2, a="A") + pair(3, 2, a="B") + pair(2, 2, a="B") + pair(a="B")
     scratch += [pltpu.VMEM((2, 640, 2048), BF16), pltpu.VMEM((2, 2048, FT), BF16)]
     scratch += [pltpu.VMEM((2,) + b.shape[2:], BF16) for b in blocks]
-    scratch += [pltpu.VMEM((2,) + b.shape[2:], F32) for b in blocks] * 2
     dma = pltpu.SemaphoreType.DMA
-    scratch += [dma((6, 40)), dma((6, 40)), dma((2,)), dma((2,)), dma((3, 3)), dma((6, 3)), pltpu.SemaphoreType.REGULAR((6,))]
+    scratch += [dma((sum(SPLIT), 40)), dma((sum(SPLIT), 40)), dma((2,)), dma((2,)), dma((3, 3)), pltpu.SemaphoreType.REGULAR((sum(SPLIT),))]
     return pl.pallas_call(
         kernel,
         in_specs=[hbm] * 19,
-        out_specs=[hbm] * 9,
+        out_specs=[pl.BlockSpec(memory_space=pltpu.VMEM)] * 9,
         out_shape=outs,
         scratch_shapes=scratch,
-        compiler_params=pltpu.CompilerParams(collective_id=0, has_side_effects=True, vmem_limit_bytes=67043328),
+        compiler_params=pltpu.CompilerParams(collective_id=0, has_side_effects=True, vmem_limit_bytes=38 * 2**20),
         cost_estimate=pl.CostEstimate(flops=6 * 2 * 2048 * 640 * 2560, bytes_accessed=100 * 2**20, transcendentals=0),
     )(*parts, *blocks, *moments)
+
+
+def put_kernel(*refs):
+    n = len(refs) // 2
+    copies = [pltpu.make_async_copy(src, dst, refs[-1].at[i]) for i, (src, dst) in enumerate(zip(refs[:n], refs[n : 2 * n]))]
+    for c in copies:
+        c.start()
+    for c in copies:
+        c.wait()
+
+
+def put(arrays):
+    return pl.pallas_call(
+        put_kernel,
+        in_specs=[pl.BlockSpec(memory_space=pltpu.VMEM)] * len(arrays),
+        out_specs=[pl.BlockSpec(memory_space=pltpu.HBM)] * len(arrays),
+        out_shape=[jax.ShapeDtypeStruct(a.shape, a.dtype) for a in arrays],
+        scratch_shapes=[pltpu.SemaphoreType.DMA((len(arrays),))],
+        compiler_params=pltpu.CompilerParams(vmem_limit_bytes=2**20),
+    )(*arrays)
 
 
 def solution(mesh):
     def step(x, dy, wg, wu, wd, *moments):
         parts = chain(x[0], dy[0], wg, wu, wd)
-        new = comm(parts, (wg, wu, wd), moments)
+        new = put(comm(parts, (wg, wu, wd), moments))
         return tuple(t.reshape(w.shape) for t, w in zip(new, (wg, wu, wd))) + tuple(new[3:])
 
     whole, rows = P(None, None, None), P(None, "dp", None)

time: 371 us -> 317 us (0.85)
  Pallas kernels: 350 us -> 316 us
  local copies, waits for them, and re-layouts: 20.2 us -> 0 us
    pallas_call x1 -> x2, Pallas kernels: 255 us -> 220 us  [the longest x1 212 us: comm(): pl.pallas_call(kernel, in_specs=[hbm] * 19, out_specs=[pl.BlockSpec(memor...]
    unnamed x27 -> x0, local copies, waits for them, and re-layouts: 20.2 us -> none
where the time goes in v2:
time: 317 us
  Pallas kernels  316 us (100%)
    pallas_call x1, Pallas kernels, comm(): pl.pallas_call(kernel, in_specs=[hbm] * 19, out_specs=[pl.BlockSpec(memor...  212 us
    pallas_call x1, Pallas kernels, chain(): pl.pallas_call(lambda *r: chain_kernel(*r, ft=ft), grid=(tokens // tile,)...  95.5 us
    pallas_call x1, Pallas kernels, put(): pl.pallas_call(put_kernel, in_specs=[pl.BlockSpec(memory_space=pltpu.VMEM...  8.31 us

profile of v2, /device:TPU:0, one launch (start us, length us, event | category | flops | bytes accessed | tf_op | source)
XLA Modules:
  0.0 316.6 jit_solution(6346516443036142771)
XLA Ops:
  0.6 95.5 %shard_map.178 = (bf16[2048,2560]{1,0:T(8,128)(2,1)}, bf16[2048,2560]{1,0:T(8,128)(2,1)}, bf16[2048,2560]{1,0:T(8,128)(2,1)}, bf16[2048,2560]{1,0:T(8,128)(2,1)}...) custom-call(bf16[2048,640]{1,0:T(8,128)(2,1)} %bitcast.14, ...), custom_call_target="tpu_custom_call" | custom-call | flops 60397977600 | bytes 104857600 | tf_op jit(solution)/shard_map/pallas_call | solution.py:109
  96.1 212.0 %shard_map.179 = (bf16[2,2,4,2,40,2560]{5,4,3,2,1,0:T(8,128)(2,1)S(1)}, bf16[2,2,4,2,40,2560]{5,4,3,2,1,0:T(8,128)(2,1)S(1)}, bf16[2,2,4,2,160,640]{5,4,3,2,1,0:...) custom-call(bf16[2048,2560]{1,0:T(8,128)(2,1)} %get-tuple-element.37, ...), custom_call_target="tpu_custom_call" | custom-call | flops 40265318400 | bytes 104857600 | tf_op jit(solution)/shard_map/pallas_call | solution.py:538
  308.1 8.3 %shard_map.180 = (bf16[2,2,4,2,40,2560]{5,4,3,2,1,0:T(8,128)(2,1)}, bf16[2,2,4,2,40,2560]{5,4,3,2,1,0:T(8,128)(2,1)}, bf16[2,2,4,2,160,640]{5,4,3,2,1,0:T(8,128)...) custom-call(bf16[2,2,4,2,40,2560]{5,4,3,2,1,0:T(8,128)(2,1)S(1)} %ge, ...), custom_call_target="tpu_custom_call" | custom-call | tf_op jit(solution)/shard_map/pallas_call | solution.py:559

commit v3 on v2

--- a/solution.py
+++ b/solution.py
@@ -119,8 +119,8 @@
 MESH = pl.DeviceIdType.MESH
 CHUNKS = (("gate", 1), ("up", 1), ("down", 1), ("gate", 0), ("up", 0), ("down", 0))
 FT = 512
-SPLIT = (1, 1, 1, 1, 1, 2)
-PERIOD, STEP, TILE = 14.0, 4.0, 1.7
+SPLIT = (2, 1, 1, 1, 1, 2)
+PERIOD, STEP, TILE = 13.0, 4.0, 1.7
 
 
 def adamw(w, m, v, g):

time: 317 us -> 310 us (0.978)
  Pallas kernels: 316 us -> 309 us
    pallas_call x1, Pallas kernels: 212 us -> 205 us  [comm(): pl.pallas_call(kernel, in_specs=[hbm] * 19, out_specs=[pl.BlockSpec(memor...]
where the time goes in v3:
time: 310 us
  Pallas kernels  309 us (100%)
    pallas_call x1, Pallas kernels, comm(): pl.pallas_call(kernel, in_specs=[hbm] * 19, out_specs=[pl.BlockSpec(memor...  205 us
    pallas_call x1, Pallas kernels, chain(): pl.pallas_call(lambda *r: chain_kernel(*r, ft=ft), grid=(tokens // tile,)...  95.5 us
    pallas_call x1, Pallas kernels, put(): pl.pallas_call(put_kernel, in_specs=[pl.BlockSpec(memory_space=pltpu.VMEM...  8.31 us

profile of v3, /device:TPU:0, one launch (start us, length us, event | category | flops | bytes accessed | tf_op | source)
XLA Modules:
  0.0 309.6 jit_solution(2960350165433302052)
XLA Ops:
  0.6 95.5 %shard_map.178 = (bf16[2048,2560]{1,0:T(8,128)(2,1)}, bf16[2048,2560]{1,0:T(8,128)(2,1)}, bf16[2048,2560]{1,0:T(8,128)(2,1)}, bf16[2048,2560]{1,0:T(8,128)(2,1)}...) custom-call(bf16[2048,640]{1,0:T(8,128)(2,1)} %bitcast.14, ...), custom_call_target="tpu_custom_call" | custom-call | flops 60397977600 | bytes 104857600 | tf_op jit(solution)/shard_map/pallas_call | solution.py:109
  96.1 205.0 %shard_map.179 = (bf16[2,2,4,2,40,2560]{5,4,3,2,1,0:T(8,128)(2,1)S(1)}, bf16[2,2,4,2,40,2560]{5,4,3,2,1,0:T(8,128)(2,1)S(1)}, bf16[2,2,4,2,160,640]{5,4,3,2,1,0:...) custom-call(bf16[2048,2560]{1,0:T(8,128)(2,1)} %get-tuple-element.37, ...), custom_call_target="tpu_custom_call" | custom-call | flops 40265318400 | bytes 104857600 | tf_op jit(solution)/shard_map/pallas_call | solution.py:538
  301.1 8.3 %shard_map.180 = (bf16[2,2,4,2,40,2560]{5,4,3,2,1,0:T(8,128)(2,1)}, bf16[2,2,4,2,40,2560]{5,4,3,2,1,0:T(8,128)(2,1)}, bf16[2,2,4,2,160,640]{5,4,3,2,1,0:T(8,128)...) custom-call(bf16[2,2,4,2,40,2560]{5,4,3,2,1,0:T(8,128)(2,1)S(1)} %ge, ...), custom_call_target="tpu_custom_call" | custom-call | tf_op jit(solution)/shard_map/pallas_call | solution.py:559

commit v4 on v3

--- a/solution.py
+++ b/solution.py
@@ -32,10 +32,13 @@
     i = pl.program_id(0)
     copies = [pltpu.make_async_copy(src.at[l], dst.at[l], sems.at[l, k]) for l in range(2) for k, (src, dst) in enumerate(((wg_hbm, wg), (wu_hbm, wu), (wd_hbm, wd)))]
 
-    @pl.when(i == 0)
-    def _():
-        for c in copies:
-            c.start()
+    def ask(*which):
+        @pl.when(i == 0)
+        def _():
+            for n in which:
+                copies[n].start()
+
+    ask(0, 1)
 
     def arrived(n):
         @pl.when(i == 0)
@@ -50,6 +53,7 @@
     dyt_ref[...] = dy.T
     arrived(0)
     arrived(1)
+    ask(2)
     total = jnp.zeros(x.shape, F32)
     for f in range(0, ff, ft):
         fs = pl.ds(f, ft)
@@ -61,6 +65,7 @@
         act1_ref[:, fs] = act
         if f == 0:
             arrived(2)
+            ask(3, 4, 5)
         total += dot(act, wd[0, fs, :])
     h = x + total.astype(BF16)
     arrived(3)

time: 310 us -> 312 us (level)
  no operation moved by 1% of the time
where the time goes in v4:
time: 312 us
  Pallas kernels  311 us (100%)
    pallas_call x1, Pallas kernels, comm(): pl.pallas_call(kernel, in_specs=[hbm] * 19, out_specs=[pl.BlockSpec(memor...  205 us
    pallas_call x1, Pallas kernels, chain(): pl.pallas_call(lambda *r: chain_kernel(*r, ft=ft), grid=(tokens // tile,)...  97.6 us
    pallas_call x1, Pallas kernels, put(): pl.pallas_call(put_kernel, in_specs=[pl.BlockSpec(memory_space=pltpu.VMEM...  8.31 us

profile of v4, /device:TPU:0, one launch (start us, length us, event | category | flops | bytes accessed | tf_op | source)
XLA Modules:
  0.0 311.9 jit_solution(11137507026998973495)
XLA Ops:
  0.6 97.6 %shard_map.178 = (bf16[2048,2560]{1,0:T(8,128)(2,1)}, bf16[2048,2560]{1,0:T(8,128)(2,1)}, bf16[2048,2560]{1,0:T(8,128)(2,1)}, bf16[2048,2560]{1,0:T(8,128)(2,1)}...) custom-call(bf16[2048,640]{1,0:T(8,128)(2,1)} %bitcast.14, ...), custom_call_target="tpu_custom_call" | custom-call | flops 60397977600 | bytes 104857600 | tf_op jit(solution)/shard_map/pallas_call | solution.py:114
  98.2 205.1 %shard_map.179 = (bf16[2,2,4,2,40,2560]{5,4,3,2,1,0:T(8,128)(2,1)S(1)}, bf16[2,2,4,2,40,2560]{5,4,3,2,1,0:T(8,128)(2,1)S(1)}, bf16[2,2,4,2,160,640]{5,4,3,2,1,0:...) custom-call(bf16[2048,2560]{1,0:T(8,128)(2,1)} %get-tuple-element.37, ...), custom_call_target="tpu_custom_call" | custom-call | flops 40265318400 | bytes 104857600 | tf_op jit(solution)/shard_map/pallas_call | solution.py:543
  303.4 8.3 %shard_map.180 = (bf16[2,2,4,2,40,2560]{5,4,3,2,1,0:T(8,128)(2,1)}, bf16[2,2,4,2,40,2560]{5,4,3,2,1,0:T(8,128)(2,1)}, bf16[2,2,4,2,160,640]{5,4,3,2,1,0:T(8,128)...) custom-call(bf16[2,2,4,2,40,2560]{5,4,3,2,1,0:T(8,128)(2,1)S(1)} %ge, ...), custom_call_target="tpu_custom_call" | custom-call | tf_op jit(solution)/shard_map/pallas_call | solution.py:564
